TPU v7x, 32 devices: a whole 2x2x4 slice. The times are simulated.
32 devices in a mesh: wave: 16 (over z, y, core), lev: 2 (over x).
Axes of the slice: x: 2, y: 2, z: 4, core: 2. Of those that a mesh axis runs over, the one named last changes fastest.
Arguments:
- control: bfloat16 [2, 256, 256, 2, 512], P(None, 'wave', 'lev'), may hold values from -6 to 6
- wave_of_slot: int32 [256], replicated, may hold values from 0 to 255, each once
- legendre: bfloat16 [256, 256, 256], P('wave', 'lev'), may hold values from -0.375 to 0.375
- vertical: bfloat16 [4, 4, 128, 128], replicated, may hold values from -0.5 to 0.5
- points: int32 [256], P('wave'), may hold values from 128 to 512
- lat_band: int32 [256], P('wave'), may hold values from 0 to 7, never falling along the last dimension, each value on 1 to 64 neighbouring positions
- grid_scale: float32 [8, 512], P(None, 'lev'), may hold values from 0.5 to 2
- obs_weight: bfloat16 [256, 512, 512], P('wave', 'lev'), may hold values from 0.19921875 to 1
Outputs:
- increment: bfloat16 [2, 256, 512, 512], P(None, 'wave', 'lev')
- gradient: bfloat16 [2, 256, 256, 2, 512], P(None, 'wave', 'lev')
Inputs may be any that keep to these rules, and one draw needn't show every extreme that they name: `wave_of_slot`: each zonal wavenumber 0 to 255 stands in exactly one slot. `lat_band`: band numbers never fall from one latitude to the next, and each band covers 1 to 64 latitudes.
All inputs are finite; a program needn't handle non-finite values.
Results may differ from a plain program's by a relative error of at most 0.007.
Values may be sent and summed in bfloat16 or wider, within the bound.
A program may use at most 192 MiB of HBM per device.

v0:
```python
import math
import jax
import jax.numpy as jnp
from jax import lax
from jax.sharding import PartitionSpec as P

WAVES = 256
LONGITUDES = 512
LEVELS = 128
VARIABLES = 4
COV_BANDS = 4


def fourier_table(wave_ids, lat_points):
    lon_index = jnp.arange(LONGITUDES, dtype=jnp.int32)
    remainder = wave_ids[None, :, None] * lon_index[None, None, :] % lat_points[:, None, None]
    angles = (
        2.0
        * math.pi
        * remainder.astype(jnp.float32)
        / lat_points.astype(jnp.float32)[:, None, None]
    )
    factor = jnp.where(wave_ids == 0, 1.0, 2.0).astype(jnp.float32) / math.sqrt(4.0 * WAVES)
    inside = lon_index[None, None, :] < lat_points[:, None, None]
    cosine = jnp.where(inside, factor[None, :, None] * jnp.cos(angles), 0.0)
    sine = jnp.where(inside, -factor[None, :, None] * jnp.sin(angles), 0.0)
    return jnp.stack([cosine, sine], axis=2).astype(jnp.bfloat16)


def vertical_apply(field, vertical, live_rows, band_of, forward):
    members, slots, rows_dev = (field.shape[0], field.shape[1], field.shape[2])
    shaped = field.reshape(members, slots, rows_dev, 2, VARIABLES, LEVELS)
    form = "eskpam,alm->eskpal" if forward else "eskpal,alm->eskpam"
    summed = jnp.zeros(shaped.shape, jnp.float32)
    for index_band in range(COV_BANDS):
        partial_value = jnp.einsum(
            form, shaped, vertical[index_band], preferred_element_type=jnp.float32
        )
        chosen = live_rows & (band_of == index_band)
        summed = summed + jnp.where(chosen[None, :, :, None, None, None], partial_value, 0.0)
    return summed.reshape(field.shape).astype(jnp.bfloat16)


def to_bands(values):
    return lax.all_to_all(values, "wave", split_axis=2, concat_axis=1, tiled=True)


def shards(control, wave_of_slot, legendre, vertical, points, lat_band, grid_scale, obs_weight):
    members, slots, rows_dev = (control.shape[0], control.shape[1], control.shape[2])
    slot_start = lax.axis_index("wave") * slots
    row_start = lax.axis_index("lev") * rows_dev
    own_waves = lax.dynamic_slice_in_dim(wave_of_slot, slot_start, slots)
    row_index = row_start + jnp.arange(rows_dev, dtype=jnp.int32)
    totals_n = own_waves[:, None] + row_index[None, :]
    live_rows = totals_n <= WAVES - 1
    band_of = jnp.minimum(totals_n * COV_BANDS // WAVES, COV_BANDS - 1)
    spectral = vertical_apply(control, vertical, live_rows, band_of, True)
    columns = lax.all_to_all(spectral, "lev", split_axis=4, concat_axis=2, tiled=True)
    col_dev = columns.shape[4]
    width = 2 * col_dev
    all_rows = columns.shape[2]
    columns = columns.reshape(members, slots, all_rows, width)
    coeffs = jnp.einsum(
        "skt,eskq->estq",
        lax.all_gather(legendre, "lev", axis=1, tiled=True),
        columns,
        preferred_element_type=jnp.float32,
    )
    coeffs = coeffs.astype(jnp.bfloat16)
    by_lat = to_bands(coeffs)
    wave_count = by_lat.shape[1]
    lat_dev = by_lat.shape[2]
    by_lat = by_lat.reshape(members, wave_count, lat_dev, 2, col_dev)
    fourier = fourier_table(wave_of_slot, points)
    synthesis = jnp.einsum("tspj,estpc->etcj", fourier, by_lat, preferred_element_type=jnp.float32)
    chooser = (
        lat_band[:, None] == jnp.arange(grid_scale.shape[0], dtype=jnp.int32)[None, :]
    ).astype(jnp.float32)
    lat_scale = jnp.dot(chooser, grid_scale, precision=lax.Precision.HIGHEST)
    increment = (synthesis * lat_scale[None, :, :, None]).astype(jnp.bfloat16)
    weighted = (
        increment.astype(jnp.float32) * obs_weight.astype(jnp.float32) * lat_scale[None, :, :, None]
    ).astype(jnp.bfloat16)
    adjoint_fourier = jnp.einsum(
        "tspj,etcj->etspc", fourier, weighted, preferred_element_type=jnp.float32
    )
    adjoint_fourier = adjoint_fourier.astype(jnp.bfloat16).reshape(
        members, lat_dev, wave_count, width
    )
    band_rows = to_bands(adjoint_fourier)
    adjoint_coeffs = jnp.einsum(
        "skt,etsq->eskq",
        lax.all_gather(legendre, "lev", axis=1, tiled=True),
        band_rows,
        preferred_element_type=jnp.float32,
    )
    adjoint_coeffs = adjoint_coeffs.astype(jnp.bfloat16).reshape(
        members, slots, all_rows, 2, col_dev
    )
    rows_back = lax.all_to_all(adjoint_coeffs, "lev", split_axis=2, concat_axis=4, tiled=True)
    gradient = vertical_apply(rows_back, vertical, live_rows, band_of, False)
    return (increment, gradient)


def solution(mesh):
    in_specs = (
        P(None, "wave", "lev", None, None),
        P(),
        P("wave", "lev", None),
        P(),
        P("wave"),
        P("wave"),
        P(None, "lev"),
        P("wave", "lev", None),
    )
    out_specs = (P(None, "wave", "lev", None), P(None, "wave", "lev", None, None))
    return jax.shard_map(shards, mesh=mesh, in_specs=in_specs, out_specs=out_specs, check_vma=False)
```

profile of v0, /device:TPU:0, one launch (start us, length us, event | category | flops | bytes accessed | tf_op | source)
XLA Modules:
  0.0 1023.2 jit_solution(5257670310123423608)
XLA Ops:
  7.2 14.1 %reshape.273 = bf16[2,16,128,2,4,128]{5,4,3,2,1,0:T(4,128)(2,1)} reshape(bf16[2,16,128,2,512]{4,3,2,1,0:T(2,128)(2,1)} %param.8) | data formatting | bytes 16777216 | tf_op jit(solution)/shard_map/reshape | solution.py:32
  21.3 11.6 %fusion.28 = f32[4,128,2,16,128,2]{4,1,5,3,2,0:T(8,128)} fusion(bf16[2,16,128,2,4,128]{5,4,3,2,1,0:T(4,128)(2,1)} %reshape.273, bf16[4,4,128,128]{3,2,1,0:T(8,128)(2,1)S(1)} %copy-done.4), kind=kOutput, calls=%fused_computation.35 | convolution fusion | flops 1073741824 | bytes 25296896 | tf_op jit(solution)/shard_map/eskpam,alm->eskpal/dot_general | solution.py:36
  49.9 23.9 %fusion.34 = bf16[2,16,128,2,4,128]{2,5,3,1,0,4:T(8,128)(2,1)} fusion(bf16[2,16,128,2,4,128]{5,4,3,2,1,0:T(4,128)(2,1)} %reshape.273, pred[16,128]{1,0:T(8,128)(4,1)S(1)} %get-tuple-element.14, f32[4,128,2,16,128,2]{4,1,5,3,2,0:T(8,128)} %fusion.28, pred[16,128]{1,0:T(8,128)(4,1)S(1)} %get-tuple-element.15, f32[4,128,2,16,128,2]{4,1,5,3,2,0:T(8,128)} %fusion.30, ...), kind=kOutput, calls=%fused_computation.41 | convolution fusion | flops 1107296256 | bytes 67248128 | tf_op jit(solution)/shard_map/eskpam,alm->eskpal/dot_general | solution.py:36
  84.3 13.1 %copy.74 = bf16[2,16,128,2,512]{2,3,1,0,4:T(2,128)(2,1)} copy(bf16[2,16,128,2,512]{2,4,3,1,0:T(8,128)(2,1)} %bitcast.123) | data formatting | bytes 16777216 | tf_op jit(solution)/shard_map/convert_element_type | solution.py:41
  105.1 115.7 %all-to-all-done = bf16[2,16,128,2,512]{2,3,1,0,4:T(2,128)(2,1)} async-done(((bf16[2,16,128,2,512]{2,3,1,0,4:T(2,128)(2,1)}), bf16[2,16,128,2,512]{2,3,1,0,4:T(2,128)(2,1)}, u32[]{:S(2)}, u32[]{:S(2)}) %all-to-all-start) | async-done | bytes 8388640 | tf_op jit(solution)/shard_map/all_to_all | solution.py:58
  220.8 16.5 %copy.75 = bf16[2,16,128,2,512]{2,4,3,1,0:T(8,128)(2,1)} copy(bf16[2,16,128,2,512]{2,3,1,0,4:T(2,128)(2,1)} %all-to-all-done) | data formatting | bytes 16777216 | tf_op jit(solution)/shard_map/all_to_all | solution.py:58
  237.3 16.8 %copy.76 = bf16[2,16,2,128,2,256]{3,2,5,4,0,1:T(2,128)(2,1)} copy(bf16[2,16,2,128,2,256]{3,5,2,4,1,0:T(8,128)(2,1)} %bitcast.124) | data formatting | bytes 16777216 | tf_op jit(solution)/shard_map/all_to_all | solution.py:58
  254.0 14.0 %reshape.274 = bf16[2,16,256,512]{2,3,0,1:T(8,128)(2,1)} reshape(bf16[2,16,2,128,2,256]{3,2,5,4,0,1:T(2,128)(2,1)} %copy.76) | data formatting | bytes 16777216 | tf_op jit(solution)/shard_map/reshape | solution.py:62
  277.8 21.1 %copy.77 = bf16[2,16,256,512]{3,0,1,2:T(2,128)(2,1)} copy(bf16[2,16,256,512]{2,3,0,1:T(8,128)(2,1)} %convert_bitcast_fusion) | data formatting | bytes 16777216 | tf_op jit(solution)/shard_map/convert_element_type | solution.py:69
  312.0 121.6 %select_convert_fusion.1 = (bf16[16,256,1,512]{3,1,2,0:T(8,128)(2,1)}, bf16[16,256,1,512]{3,1,2,0:T(8,128)(2,1)}) fusion(f32[256]{0:T(256)S(1)} %get-tuple-element.16, f32[16]{0:T(128)S(1)} %get-tuple-element.19, pred[16]{0:T(512)(128)(4,1)S(1)} %broadcast_compare_fusion, s32[16]{0:T(128)S(1)} %get-tuple-element.18, s32[256,512]{1,0:T(8,128)S(1)} %iota_multiply_fusion, ...), kind=kLoop, calls=%fused_computation.21 | loop fusion | flops 33554432 | bytes 8923280 | tf_op jit(solution)/shard_map/convert.1
  433.6 21.9 %all-to-all-done.1 = bf16[2,16,256,512]{3,0,1,2:T(2,128)(2,1)} async-done(((bf16[2,16,256,512]{3,0,1,2:T(2,128)(2,1)}), bf16[2,16,256,512]{3,0,1,2:T(2,128)(2,1)}, u32[]{:S(2)}, u32[]{:S(2)}) %all-to-all-start.1) | async-done | bytes 8388640 | tf_op jit(solution)/shard_map/all_to_all | solution.py:45
  475.3 12.5 %reshape.275 = bf16[2,256,16,2,256]{4,3,2,1,0:T(2,128)(2,1)} reshape(bf16[2,16,16,16,512]{4,3,2,1,0:T(8,128)(2,1)} %copy.79) | data formatting | bytes 16777216 | tf_op jit(solution)/shard_map/reshape | solution.py:73
  487.8 17.3 %fusion.40 = bf16[2,16,256,512]{3,2,0,1:T(8,128)(2,1)} fusion(f32[16,256]{1,0:T(8,128)S(1)} %fusion.73, bf16[16,256,1,512]{3,1,2,0:T(8,128)(2,1)} %get-tuple-element.11, bf16[16,256,1,512]{3,1,2,0:T(8,128)(2,1)} %get-tuple-element.10, bf16[2,256,16,2,256]{4,3,2,1,0:T(2,128)(2,1)} %reshape.275), kind=kOutput, calls=%fused_computation.43 | convolution fusion | flops 4307550208 | bytes 25182208 | tf_op jit(solution)/shard_map/tspj,estpc->etcj/dot_general | solution.py:75
  505.0 13.4 %fusion.17 = bf16[16,2,256,256,2]{3,2,4,1,0:T(8,128)(2,1)} fusion(bf16[2,16,256,512]{3,2,0,1:T(8,128)(2,1)} %fusion.40, f32[16,256]{1,0:T(8,128)S(1)} %fusion.73, f32[16,256,512]{2,1,0:T(8,128)} %convert_element_type.68, bf16[16,256,1,512]{3,1,2,0:T(8,128)(2,1)} %get-tuple-element.11, bf16[16,256,1,512]{3,1,2,0:T(8,128)(2,1)} %get-tuple-element.10), kind=kOutput, calls=%fused_computation.26 | convolution fusion | flops 4332716032 | bytes 33570816 | tf_op jit(solution)/shard_map/tspj,etcj->etspc/dot_general | solution.py:84
  518.5 14.6 %copy.81 = bf16[2,16,256,512]{3,1,0,2:T(8,128)(2,1)} copy(bf16[2,16,256,512]{2,3,0,1:T(8,128)(2,1)} %bitcast.129) | data formatting | bytes 16777216 | tf_op jit(solution)/shard_map/reshape | solution.py:87
  533.0 218.6 %all_to_all.63 = bf16[2,16,256,512]{3,1,0,2:T(8,128)(2,1)} all-to-all(bf16[2,16,256,512]{3,1,0,2:T(8,128)(2,1)} %copy.81), channel_id=1, replica_groups=mesh['wave'=16,'lev'=2] {'wave'}, dimensions={2} | all-to-all | bytes 16777216 | tf_op jit(solution)/shard_map/all_to_all | solution.py:45
  751.6 15.5 %copy.83 = bf16[2,16,16,16,512]{4,3,2,1,0:T(8,128)(2,1)} copy(bf16[2,16,16,16,512]{4,2,0,3,1:T(8,128)(2,1)} %bitcast.126) | data formatting | bytes 16777216 | tf_op jit(solution)/shard_map/all_to_all | solution.py:45
  767.1 12.7 %fusion.14 = bf16[16,2,512,256]{3,2,1,0:T(8,128)(2,1)} fusion(bf16[2,256,16,512]{3,2,1,0:T(8,128)(2,1)} %bitcast.121, bf16[16,256,256]{2,1,0:T(8,128)(2,1)S(1)} %copy-done.3), kind=kOutput, calls=%fused_computation.25 | convolution fusion | flops 2151677952 | bytes 18874368 | tf_op jit(solution)/shard_map/skt,etsq->eskq/dot_general | solution.py:91
  779.7 21.1 %copy.85 = bf16[2,16,256,2,256]{4,3,1,0,2:T(2,128)(2,1)} copy(bf16[2,16,256,2,256]{2,4,3,0,1:T(8,128)(2,1)} %bitcast.122) | data formatting | bytes 16777216 | tf_op jit(solution)/shard_map/reshape | solution.py:97
  815.5 86.1 %all-to-all-done.3 = bf16[2,16,256,2,256]{4,3,1,0,2:T(2,128)(2,1)} async-done(((bf16[2,16,256,2,256]{4,3,1,0,2:T(2,128)(2,1)}), bf16[2,16,256,2,256]{4,3,1,0,2:T(2,128)(2,1)}, u32[]{:S(2)}, u32[]{:S(2)}) %all-to-all-start.3) | async-done | bytes 8388640 | tf_op jit(solution)/shard_map/all_to_all | solution.py:100
  901.5 13.6 %copy.86 = bf16[2,16,256,2,256]{4,2,3,1,0:T(8,128)(2,1)} copy(bf16[2,16,256,2,256]{4,3,1,0,2:T(2,128)(2,1)} %all-to-all-done.3) | data formatting | bytes 16777216 | tf_op jit(solution)/shard_map/all_to_all | solution.py:100
  915.2 12.1 %copy.87 = bf16[2,16,128,2,2,256]{2,5,4,3,1,0:T(8,128)(2,1)} copy(bf16[2,16,128,2,2,256]{5,2,4,3,1,0:T(8,128)(2,1)} %bitcast.127) | data formatting | bytes 16777216 | tf_op jit(solution)/shard_map/all_to_all | solution.py:100
  961.7 23.0 %fusion.37 = bf16[2,16,128,2,4,128]{2,5,3,1,0,4:T(8,128)(2,1)} fusion(bf16[2,16,128,2,4,128]{2,5,4,3,1,0:T(8,128)(2,1)} %bitcast.120, pred[16,128]{1,0:T(8,128)(4,1)S(1)} %copy-done.10, f32[4,2,16,128,2,128]{3,5,4,2,1,0:T(8,128)} %fusion.21, pred[16,128]{1,0:T(8,128)(4,1)S(1)} %copy-done.12, f32[4,2,16,128,2,128]{3,5,4,2,1,0:T(8,128)} %fusion.23, ...), kind=kOutput, calls=%fused_computation.42 | convolution fusion | flops 1107296256 | bytes 67248128 | tf_op jit(solution)/shard_map/eskpal,alm->eskpam/dot_general | solution.py:36
  995.1 21.1 %copy.98 = bf16[2,16,128,2,512]{4,3,2,1,0:T(2,128)(2,1)} copy(bf16[2,16,128,2,512]{2,4,3,1,0:T(8,128)(2,1)} %bitcast.128) | data formatting | bytes 16777216
  (59 shorter events, 137.2 us)
Async XLA Ops:
  7.2 304.5 %copy-start = (f32[8,256]{1,0:T(8,128)S(1)}, f32[8,256]{1,0:T(8,128)}, u32[]{:S(2)}) copy-start(f32[8,256]{1,0:T(8,128)} %param.14) | copy-start | bytes 24580
  7.2 14.1 %copy-start.4 = (bf16[4,4,128,128]{3,2,1,0:T(8,128)(2,1)S(1)}, bf16[4,4,128,128]{3,2,1,0:T(8,128)(2,1)}, u32[]{:S(2)}) copy-start(bf16[4,4,128,128]{3,2,1,0:T(8,128)(2,1)} %param.11) | copy-start | bytes 1572868
  21.3 11.6 %copy-start.2 = (bf16[2,16,128,2,4,128]{5,4,3,2,1,0:T(4,128)(2,1)S(1)}, bf16[2,16,128,2,4,128]{5,4,3,2,1,0:T(4,128)(2,1)}, u32[]{:S(2)}) copy-start(bf16[2,16,128,2,4,128]{5,4,3,2,1,0:T(4,128)(2,1)} %reshape.273) | copy-start | bytes 25165828
  41.0 8.1 copy-start.13
  49.3 0.6 copy-start.5
  49.3 0.6 copy-start.7
  49.3 0.6 copy-start.9
  49.3 0.6 copy-start.11
  97.5 123.3 %all-to-all-start = ((bf16[2,16,128,2,512]{2,3,1,0,4:T(2,128)(2,1)}), bf16[2,16,128,2,512]{2,3,1,0,4:T(2,128)(2,1)}, u32[]{:S(2)}, u32[]{:S(2)}) async-start(bf16[2,16,128,2,512]{2,3,1,0,4:T(2,128)(2,1)} %copy.74), calls=%async_computation | async-start | bytes 16777216 | tf_op jit(solution)/shard_map/all_to_all | solution.py:58
  104.4 163.7 %all-gather.2.cloned.1.call-start = ((), (), s32[]{:S(2)}) async-start(), calls=%async_computation.4 | async-start | bytes 3145728 | tf_op jit(solution)/shard_map/all_gather | solution.py:65
  298.8 156.7 %all-to-all-start.1 = ((bf16[2,16,256,512]{3,0,1,2:T(2,128)(2,1)}), bf16[2,16,256,512]{3,0,1,2:T(2,128)(2,1)}, u32[]{:S(2)}, u32[]{:S(2)}) async-start(bf16[2,16,256,512]{3,0,1,2:T(2,128)(2,1)} %copy.77), calls=%async_computation.1 | async-start | bytes 16777216 | tf_op jit(solution)/shard_map/all_to_all | solution.py:45
  305.0 6.6 copy-start.14
  305.0 6.7 copy-start.15
  751.6 15.5 %copy-start.3 = (bf16[16,256,256]{2,1,0:T(8,128)(2,1)S(1)}, bf16[16,256,256]{2,1,0:T(8,128)(2,1)}, u32[]{:S(2)}) copy-start(bf16[16,256,256]{2,1,0:T(8,128)(2,1)} %all-gather.2.cloned.1.call-done) | copy-start | bytes 6291460
  800.8 100.7 %all-to-all-start.3 = ((bf16[2,16,256,2,256]{4,3,1,0,2:T(2,128)(2,1)}), bf16[2,16,256,2,256]{4,3,1,0,2:T(2,128)(2,1)}, u32[]{:S(2)}, u32[]{:S(2)}) async-start(bf16[2,16,256,2,256]{4,3,1,0,2:T(2,128)(2,1)} %copy.85), calls=%async_computation.3 | async-start | bytes 16777216 | tf_op jit(solution)/shard_map/all_to_all | solution.py:100
  950.2 11.5 %copy-start.6 = (pred[16,128]{1,0:T(8,128)(4,1)S(1)}, pred[16,128]{1,0:T(8,128)(4,1)}, u32[]{:S(2)}) copy-start(pred[16,128]{1,0:T(8,128)(4,1)} %copy-done.5) | copy-start | bytes 6148
  950.2 11.5 %copy-start.8 = (pred[16,128]{1,0:T(8,128)(4,1)S(1)}, pred[16,128]{1,0:T(8,128)(4,1)}, u32[]{:S(2)}) copy-start(pred[16,128]{1,0:T(8,128)(4,1)} %copy-done.7) | copy-start | bytes 6148
  950.2 11.5 %copy-start.10 = (pred[16,128]{1,0:T(8,128)(4,1)S(1)}, pred[16,128]{1,0:T(8,128)(4,1)}, u32[]{:S(2)}) copy-start(pred[16,128]{1,0:T(8,128)(4,1)} %copy-done.9) | copy-start | bytes 6148
  950.2 11.5 %copy-start.12 = (pred[16,128]{1,0:T(8,128)(4,1)S(1)}, pred[16,128]{1,0:T(8,128)(4,1)}, u32[]{:S(2)}) copy-start(pred[16,128]{1,0:T(8,128)(4,1)} %copy-done.11) | copy-start | bytes 6148
  995.1 21.1 %copy-start.1 = (f32[8,256]{1,0:T(8,128)S(1)}, f32[8,256]{1,0:T(8,128)}, u32[]{:S(2)}) copy-start(f32[8,256]{1,0:T(8,128)} %param.14) | copy-start | bytes 24580
Sparse Core Ops, SparseCore 0:
  106.8 58.8 all-gather.1
where the time goes:
time: 1030 us; the launch traced here: 1020 us
  local copies, waits for them, and re-layouts  255 us (25%)
  waiting for transfers between devices  224 us (22%)
  blocking collectives  219 us (21%)
  matrix products  162 us (16%)
  other arithmetic  128 us (12%)
  starting transfers between devices  20.1 us (2%)
  between operations  14.4 us (1%)
    all_to_all x1, blocking collectives, to_bands(): lax.all_to_all(values, 'wave', split_axis=2, concat_axis=1, tiled=True)  219 us
    another operation x1, other arithmetic  122 us
    all_to_all x1, waiting for transfers between devices, shards(): lax.all_to_all(spectral, 'lev', split_axis=4, concat_axis=2, tiled=True)  116 us
    dot_general x8, matrix products, vertical_apply(): jnp.einsum(form, shaped, vertical[index_band], preferred_element_type=jnp...  109 us
    all_to_all x1, waiting for transfers between devices, shards(): lax.all_to_all(adjoint_coeffs, 'lev', split_axis=2, concat_axis=4, tiled=...  86.1 us
    all_to_all x3, local copies, waits for them, and re-layouts, to_bands(): lax.all_to_all(values, 'wave', split_axis=2, concat_axis=1, tiled=True)  35.2 us
    all_to_all x2, local copies, waits for them, and re-layouts, shards(): lax.all_to_all(spectral, 'lev', split_axis=4, concat_axis=2, tiled=True)  33.2 us
    unnamed x34, local copies, waits for them, and re-layouts  29.4 us
  transfers between devices with their start and end apart: 4, of which 3 were waited for; matrix products, arithmetic and copies ran while one was open for 18% of the time, Pallas kernels for 0%

commit v1 on v0

--- a/solution.py
+++ b/solution.py
@@ -42,7 +42,10 @@
 
 
 def to_bands(values):
-    return lax.all_to_all(values, "wave", split_axis=2, concat_axis=1, tiled=True)
+    return jnp.concatenate(
+        lax.all_to_all(jnp.stack(jnp.split(values, lax.axis_size("wave"), axis=2)), "wave", 0, 0),
+        axis=1,
+    )
 
 
 def shards(control, wave_of_slot, legendre, vertical, points, lat_band, grid_scale, obs_weight):

time: 1030 us -> 1120 us (1.087)
  local copies, waits for them, and re-layouts: 255 us -> 335 us
    unnamed x34 -> x89, local copies, waits for them, and re-layouts: 29.4 us -> 117 us
    split x0 -> x1, local copies, waits for them, and re-layouts: none -> 48.6 us  [to_bands(): jnp.split(values, lax.axis_size('wave'), axis=2)]
    reshape x2 -> x0, local copies, waits for them, and re-layouts: 27 us -> none  [the longest x1 14.6 us: shards(): adjoint_fourier.astype(jnp.bfloat16)]
    all_to_all x3 -> x1, local copies, waits for them, and re-layouts: 35.2 us -> 8.52 us  [to_bands(): lax.all_to_all(jnp.stack(jnp.split(values, lax.axis_size('wave'), axis=2)...]
    convert_element_type x1 -> x0, local copies, waits for them, and re-layouts: 21.1 us -> none  [shards(): coeffs = coeffs.astype(jnp.bfloat16)]
    another operation x0 -> x3, local copies, waits for them, and re-layouts: none -> 13.3 us  [the longest x1 12.5 us: shards(): by_lat = by_lat.reshape(members, wave_count, lat_dev, 2, col_dev)]
  transfers between devices with their start and end apart: 4 -> 4, of which waited for: 3 -> 3; matrix products, arithmetic and copies ran while one was open for 18% -> 17% of each run, Pallas kernels for 0% -> 0%
where the time goes in v1:
time: 1120 us; the launch traced here: 1110 us
  local copies, waits for them, and re-layouts  335 us (30%)
  waiting for transfers between devices  224 us (20%)
  blocking collectives  219 us (20%)
  matrix products  167 us (15%)
  other arithmetic  127 us (11%)
  starting transfers between devices  20.5 us (2%)
  between operations  14.6 us (1%)
    all_to_all x1, blocking collectives, to_bands(): lax.all_to_all(jnp.stack(jnp.split(values, lax.axis_size('wave'), axis=2)...  219 us
    another operation x1, other arithmetic  120 us
    unnamed x89, local copies, waits for them, and re-layouts  117 us
    all_to_all x1, waiting for transfers between devices, shards(): lax.all_to_all(spectral, 'lev', split_axis=4, concat_axis=2, tiled=True)  115 us
    dot_general x8, matrix products, vertical_apply(): jnp.einsum(form, shaped, vertical[index_band], preferred_element_type=jnp...  109 us
    all_to_all x1, waiting for transfers between devices, shards(): lax.all_to_all(adjoint_coeffs, 'lev', split_axis=2, concat_axis=4, tiled=...  86.1 us
    split x1, local copies, waits for them, and re-layouts, to_bands(): jnp.split(values, lax.axis_size('wave'), axis=2)  48.6 us
    all_to_all x2, local copies, waits for them, and re-layouts, shards(): lax.all_to_all(spectral, 'lev', split_axis=4, concat_axis=2, tiled=True)  37.6 us
  transfers between devices with their start and end apart: 4, of which 3 were waited for; matrix products, arithmetic and copies ran while one was open for 17% of the time, Pallas kernels for 0%

profile of v1, /device:TPU:0, one launch (start us, length us, event | category | flops | bytes accessed | tf_op | source)
XLA Modules:
  0.0 1107.3 jit_solution(6117608717691415548)
XLA Ops:
  7.2 14.1 %reshape.278 = bf16[2,16,128,2,4,128]{5,4,3,2,1,0:T(4,128)(2,1)} reshape(bf16[2,16,128,2,512]{4,3,2,1,0:T(2,128)(2,1)} %param.8) | data formatting | bytes 16777216 | tf_op jit(solution)/shard_map/reshape | solution.py:32
  21.3 11.6 %fusion.30 = f32[4,128,2,16,128,2]{4,1,5,3,2,0:T(8,128)} fusion(bf16[2,16,128,2,4,128]{5,4,3,2,1,0:T(4,128)(2,1)} %reshape.278, bf16[4,4,128,128]{3,2,1,0:T(8,128)(2,1)S(1)} %copy-done.4), kind=kOutput, calls=%fused_computation.37 | convolution fusion | flops 1073741824 | bytes 25296896 | tf_op jit(solution)/shard_map/eskpam,alm->eskpal/dot_general | solution.py:36
  49.9 23.9 %fusion.34 = bf16[2,16,128,2,4,128]{2,5,3,1,0,4:T(8,128)(2,1)} fusion(bf16[2,16,128,2,4,128]{5,4,3,2,1,0:T(4,128)(2,1)} %reshape.278, pred[16,128]{1,0:T(8,128)(4,1)S(1)} %get-tuple-element.30, f32[4,128,2,16,128,2]{4,1,5,3,2,0:T(8,128)} %fusion.28, pred[16,128]{1,0:T(8,128)(4,1)S(1)} %get-tuple-element.31, f32[4,128,2,16,128,2]{4,1,5,3,2,0:T(8,128)} %fusion.30, ...), kind=kOutput, calls=%fused_computation.41 | convolution fusion | flops 1107296256 | bytes 67248128 | tf_op jit(solution)/shard_map/eskpam,alm->eskpal/dot_general | solution.py:36
  84.3 13.1 %copy.104 = bf16[2,16,128,2,512]{2,3,1,0,4:T(2,128)(2,1)} copy(bf16[2,16,128,2,512]{2,4,3,1,0:T(8,128)(2,1)} %bitcast.222) | data formatting | bytes 16777216 | tf_op jit(solution)/shard_map/convert_element_type | solution.py:41
  106.0 115.0 %all-to-all-done = bf16[2,16,128,2,512]{2,3,1,0,4:T(2,128)(2,1)} async-done(((bf16[2,16,128,2,512]{2,3,1,0,4:T(2,128)(2,1)}), bf16[2,16,128,2,512]{2,3,1,0,4:T(2,128)(2,1)}, u32[]{:S(2)}, u32[]{:S(2)}) %all-to-all-start) | async-done | bytes 8388640 | tf_op jit(solution)/shard_map/all_to_all | solution.py:61
  221.0 16.5 %copy.105 = bf16[2,16,128,2,512]{2,4,3,1,0:T(8,128)(2,1)} copy(bf16[2,16,128,2,512]{2,3,1,0,4:T(2,128)(2,1)} %all-to-all-done) | data formatting | bytes 16777216 | tf_op jit(solution)/shard_map/all_to_all | solution.py:61
  237.4 21.1 %copy.106 = bf16[2,16,2,128,2,256]{5,4,3,2,0,1:T(2,128)(2,1)} copy(bf16[2,16,2,128,2,256]{3,5,2,4,1,0:T(8,128)(2,1)} %bitcast.223) | data formatting | bytes 16777216 | tf_op jit(solution)/shard_map/all_to_all | solution.py:61
  258.5 14.4 %reshape.279 = bf16[2,16,256,512]{3,2,0,1:T(8,128)(2,1)} reshape(bf16[2,16,2,128,2,256]{5,4,3,2,0,1:T(2,128)(2,1)} %copy.106) | data formatting | bytes 16777216 | tf_op jit(solution)/shard_map/reshape | solution.py:65
  306.0 120.4 %select_convert_fusion.1 = (bf16[16,256,1,512]{3,1,2,0:T(8,128)(2,1)}, bf16[16,256,1,512]{3,1,2,0:T(8,128)(2,1)}) fusion(f32[256]{0:T(256)S(1)} %get-tuple-element.32, f32[16]{0:T(128)S(1)} %get-tuple-element.35, pred[16]{0:T(512)(128)(4,1)S(1)} %broadcast_compare_fusion, s32[16]{0:T(128)S(1)} %get-tuple-element.34, s32[256,512]{1,0:T(8,128)S(1)} %iota_multiply_fusion, ...), kind=kLoop, calls=%fused_computation.21 | loop fusion | flops 33554432 | bytes 8923280 | tf_op jit(solution)/shard_map/convert.1
  426.4 23.0 %all-to-all-done.1 = bf16[16,2,16,16,512]{4,3,1,2,0:T(8,128)(2,1)} async-done(((bf16[16,2,16,16,512]{4,3,1,2,0:T(8,128)(2,1)}), bf16[16,2,16,16,512]{4,3,1,2,0:T(8,128)(2,1)}, u32[]{:S(2)}, u32[]{:S(2)}) %all-to-all-start.1) | async-done | bytes 8388640 | tf_op jit(solution)/shard_map/all_to_all | solution.py:46
  449.3 12.5 %reshape_reshape.3 = bf16[2,256,16,2,256]{4,3,2,0,1:T(2,128)(2,1)} reshape(bf16[2,16,16,16,512]{4,3,0,2,1:T(8,128)(2,1)} %bitcast.35) | data formatting | bytes 16777216 | tf_op jit(solution)/shard_map/reshape;reshape | solution.py:76
  461.8 21.3 %fusion.40 = bf16[2,16,256,512]{3,2,0,1:T(8,128)(2,1)} fusion(f32[16,256]{1,0:T(8,128)S(1)} %fusion.89, bf16[16,256,1,512]{3,1,2,0:T(8,128)(2,1)} %get-tuple-element.27, bf16[16,256,1,512]{3,1,2,0:T(8,128)(2,1)} %get-tuple-element.26, bf16[2,256,16,2,256]{4,3,2,0,1:T(2,128)(2,1)} %reshape_reshape.3), kind=kOutput, calls=%fused_computation.43 | convolution fusion | flops 4307550208 | bytes 25182208 | tf_op jit(solution)/shard_map/tspj,estpc->etcj/dot_general | solution.py:78
  483.1 13.0 %fusion.17 = bf16[16,2,256,256,2]{3,2,4,1,0:T(8,128)(2,1)} fusion(bf16[2,16,256,512]{3,2,0,1:T(8,128)(2,1)} %fusion.40, f32[16,256]{1,0:T(8,128)S(1)} %fusion.89, f32[16,256,512]{2,1,0:T(8,128)} %convert_element_type.68, bf16[16,256,1,512]{3,1,2,0:T(8,128)(2,1)} %get-tuple-element.27, bf16[16,256,1,512]{3,1,2,0:T(8,128)(2,1)} %get-tuple-element.26), kind=kOutput, calls=%fused_computation.26 | convolution fusion | flops 4332716032 | bytes 33570816 | tf_op jit(solution)/shard_map/tspj,etcj->etspc/dot_general | solution.py:87
  496.1 48.6 %fusion.95 = (bf16[2,16,16,512]{2,3,0,1:T(8,128)(2,1)}, bf16[2,16,16,512]{2,3,0,1:T(8,128)(2,1)}, bf16[2,16,16,512]{2,3,0,1:T(8,128)(2,1)}, bf16[2,16,16,512]{2,...) fusion(bf16[2,16,256,512]{2,3,0,1:T(8,128)(2,1)} %bitcast.215), kind=kLoop, calls=%fused_computation.141 | loop fusion | bytes 16777216 | tf_op jit(solution)/shard_map/split | solution.py:46
  619.3 218.8 %all_to_all.40 = bf16[16,2,16,16,512]{4,3,2,1,0:T(8,128)(2,1)} all-to-all(bf16[16,2,16,16,512]{4,3,2,1,0:T(8,128)(2,1)S(1)} %bitcast_dynamic-update-slice_fusion), channel_id=1, replica_groups=mesh['wave'=16,'lev'=2] {'wave'}, dimensions={0} | all-to-all | bytes 16777216 | tf_op jit(solution)/shard_map/all_to_all | solution.py:46
  846.6 17.0 %fusion.14 = bf16[16,2,512,256]{3,2,1,0:T(8,128)(2,1)} fusion(bf16[2,256,16,512]{3,2,1,0:T(8,128)(2,1)} %bitcast.220, bf16[16,256,256]{1,2,0:T(8,128)(2,1)S(1)} %copy-done.3), kind=kOutput, calls=%fused_computation.25 | convolution fusion | flops 2151677952 | bytes 18874368 | tf_op jit(solution)/shard_map/skt,etsq->eskq/dot_general | solution.py:94
  863.6 21.1 %copy.128 = bf16[2,16,256,2,256]{4,3,1,0,2:T(2,128)(2,1)} copy(bf16[2,16,256,2,256]{2,4,3,0,1:T(8,128)(2,1)} %bitcast.221) | data formatting | bytes 16777216 | tf_op jit(solution)/shard_map/reshape | solution.py:100
  899.5 86.1 %all-to-all-done.3 = bf16[2,16,256,2,256]{4,3,1,0,2:T(2,128)(2,1)} async-done(((bf16[2,16,256,2,256]{4,3,1,0,2:T(2,128)(2,1)}), bf16[2,16,256,2,256]{4,3,1,0,2:T(2,128)(2,1)}, u32[]{:S(2)}, u32[]{:S(2)}) %all-to-all-start.3) | async-done | bytes 8388640 | tf_op jit(solution)/shard_map/all_to_all | solution.py:103
  985.6 13.6 %copy.129 = bf16[2,16,256,2,256]{4,2,3,1,0:T(8,128)(2,1)} copy(bf16[2,16,256,2,256]{4,3,1,0,2:T(2,128)(2,1)} %all-to-all-done.3) | data formatting | bytes 16777216 | tf_op jit(solution)/shard_map/all_to_all | solution.py:103
  999.2 12.1 %copy.130 = bf16[2,16,128,2,2,256]{2,5,4,3,1,0:T(8,128)(2,1)} copy(bf16[2,16,128,2,2,256]{5,2,4,3,1,0:T(8,128)(2,1)} %bitcast.224) | data formatting | bytes 16777216 | tf_op jit(solution)/shard_map/all_to_all | solution.py:103
  1011.3 11.5 %fusion.23 = f32[4,2,16,128,2,128]{3,5,4,2,1,0:T(8,128)} fusion(bf16[2,16,128,2,4,128]{2,5,4,3,1,0:T(8,128)(2,1)} %bitcast.216, bf16[4,4,128,128]{3,2,1,0:T(8,128)(2,1)S(1)} %copy-done.5), kind=kOutput, calls=%fused_computation.30 | convolution fusion | flops 1073741824 | bytes 25296896 | tf_op jit(solution)/shard_map/eskpal,alm->eskpam/dot_general | solution.py:36
  1022.8 11.5 %fusion.21 = f32[4,2,16,128,2,128]{3,5,4,2,1,0:T(8,128)} fusion(bf16[2,16,128,2,4,128]{2,5,4,3,1,0:T(8,128)(2,1)} %bitcast.217, bf16[4,4,128,128]{3,2,1,0:T(8,128)(2,1)S(1)} %copy-done.5), kind=kOutput, calls=%fused_computation.28 | convolution fusion | flops 1073741824 | bytes 25296896 | tf_op jit(solution)/shard_map/eskpal,alm->eskpam/dot_general | solution.py:36
  1045.8 23.0 %fusion.37 = bf16[2,16,128,2,4,128]{2,5,3,1,0,4:T(8,128)(2,1)} fusion(bf16[2,16,128,2,4,128]{2,5,4,3,1,0:T(8,128)(2,1)} %bitcast.219, pred[16,128]{1,0:T(8,128)(4,1)S(1)} %copy-done.14, f32[4,2,16,128,2,128]{3,5,4,2,1,0:T(8,128)} %fusion.21, pred[16,128]{1,0:T(8,128)(4,1)S(1)} %copy-done.16, f32[4,2,16,128,2,128]{3,5,4,2,1,0:T(8,128)} %fusion.23, ...), kind=kOutput, calls=%fused_computation.42 | convolution fusion | flops 1107296256 | bytes 67248128 | tf_op jit(solution)/shard_map/eskpal,alm->eskpam/dot_general | solution.py:36
  1079.2 21.1 %copy.141 = bf16[2,16,128,2,512]{4,3,2,1,0:T(2,128)(2,1)} copy(bf16[2,16,128,2,512]{2,4,3,1,0:T(8,128)(2,1)} %bitcast.225) | data formatting | bytes 16777216
  (113 shorter events, 188.5 us)
Async XLA Ops:
  7.2 298.5 %copy-start = (f32[8,256]{1,0:T(8,128)S(1)}, f32[8,256]{1,0:T(8,128)}, u32[]{:S(2)}) copy-start(f32[8,256]{1,0:T(8,128)} %param.14) | copy-start | bytes 24580
  7.2 14.1 %copy-start.4 = (bf16[4,4,128,128]{3,2,1,0:T(8,128)(2,1)S(1)}, bf16[4,4,128,128]{3,2,1,0:T(8,128)(2,1)}, u32[]{:S(2)}) copy-start(bf16[4,4,128,128]{3,2,1,0:T(8,128)(2,1)} %param.11) | copy-start | bytes 1572868
  21.3 11.7 %copy-start.2 = (bf16[2,16,128,2,4,128]{5,4,3,2,1,0:T(4,128)(2,1)S(1)}, bf16[2,16,128,2,4,128]{5,4,3,2,1,0:T(4,128)(2,1)}, u32[]{:S(2)}) copy-start(bf16[2,16,128,2,4,128]{5,4,3,2,1,0:T(4,128)(2,1)} %reshape.278) | copy-start | bytes 25165828
  41.0 8.1 copy-start.17
  49.3 0.6 copy-start.9
  49.3 0.6 copy-start.11
  49.3 0.6 copy-start.13
  49.3 0.6 copy-start.15
  97.5 7.2 copy-start.8
  97.5 123.5 %all-to-all-start = ((bf16[2,16,128,2,512]{2,3,1,0,4:T(2,128)(2,1)}), bf16[2,16,128,2,512]{2,3,1,0,4:T(2,128)(2,1)}, u32[]{:S(2)}, u32[]{:S(2)}) async-start(bf16[2,16,128,2,512]{2,3,1,0,4:T(2,128)(2,1)} %copy.104), calls=%async_computation | async-start | bytes 16777216 | tf_op jit(solution)/shard_map/all_to_all | solution.py:61
  104.6 168.4 %all-gather.2.cloned.1.call-start = ((), (), s32[]{:S(2)}) async-start(), calls=%async_computation.4 | async-start | bytes 3145728 | tf_op jit(solution)/shard_map/all_gather | solution.py:68
  292.6 156.7 %all-to-all-start.1 = ((bf16[16,2,16,16,512]{4,3,1,2,0:T(8,128)(2,1)}), bf16[16,2,16,16,512]{4,3,1,2,0:T(8,128)(2,1)}, u32[]{:S(2)}, u32[]{:S(2)}) async-start(bf16[16,2,16,16,512]{4,3,1,2,0:T(8,128)(2,1)} %fusion.45), calls=%async_computation.1 | async-start | bytes 16777216 | tf_op jit(solution)/shard_map/all_to_all | solution.py:46
  298.8 6.8 copy-start.18
  298.8 6.9 copy-start.19
  610.1 8.7 copy-start.7
  610.1 8.8 copy-start.6
  838.1 8.5 copy-start.3
  884.7 100.9 %all-to-all-start.3 = ((bf16[2,16,256,2,256]{4,3,1,0,2:T(2,128)(2,1)}), bf16[2,16,256,2,256]{4,3,1,0,2:T(2,128)(2,1)}, u32[]{:S(2)}, u32[]{:S(2)}) async-start(bf16[2,16,256,2,256]{4,3,1,0,2:T(2,128)(2,1)} %copy.128), calls=%async_computation.3 | async-start | bytes 16777216 | tf_op jit(solution)/shard_map/all_to_all | solution.py:103
  999.2 12.1 %copy-start.5 = (bf16[4,4,128,128]{3,2,1,0:T(8,128)(2,1)S(1)}, bf16[4,4,128,128]{3,2,1,0:T(8,128)(2,1)}, u32[]{:S(2)}) copy-start(bf16[4,4,128,128]{3,2,1,0:T(8,128)(2,1)} %param.11) | copy-start | bytes 1572868
  1034.3 11.5 %copy-start.10 = (pred[16,128]{1,0:T(8,128)(4,1)S(1)}, pred[16,128]{1,0:T(8,128)(4,1)}, u32[]{:S(2)}) copy-start(pred[16,128]{1,0:T(8,128)(4,1)} %copy-done.9) | copy-start | bytes 6148
  1034.3 11.5 %copy-start.12 = (pred[16,128]{1,0:T(8,128)(4,1)S(1)}, pred[16,128]{1,0:T(8,128)(4,1)}, u32[]{:S(2)}) copy-start(pred[16,128]{1,0:T(8,128)(4,1)} %copy-done.11) | copy-start | bytes 6148
  1034.3 11.5 %copy-start.14 = (pred[16,128]{1,0:T(8,128)(4,1)S(1)}, pred[16,128]{1,0:T(8,128)(4,1)}, u32[]{:S(2)}) copy-start(pred[16,128]{1,0:T(8,128)(4,1)} %copy-done.13) | copy-start | bytes 6148
  1034.3 11.5 %copy-start.16 = (pred[16,128]{1,0:T(8,128)(4,1)S(1)}, pred[16,128]{1,0:T(8,128)(4,1)}, u32[]{:S(2)}) copy-start(pred[16,128]{1,0:T(8,128)(4,1)} %copy-done.15) | copy-start | bytes 6148
  1079.2 21.1 %copy-start.1 = (f32[8,256]{1,0:T(8,128)S(1)}, f32[8,256]{1,0:T(8,128)}, u32[]{:S(2)}) copy-start(f32[8,256]{1,0:T(8,128)} %param.14) | copy-start | bytes 24580
Sparse Core Ops, SparseCore 0:
  106.9 58.8 all-gather.1
